TPU v7x, 32 devices: a whole 2x2x4 slice. The times are simulated.
32 devices in a mesh: tm: 4 (over x, core), batch: 8 (over z, y).
Axes of the slice: x: 2, y: 2, z: 4, core: 2. Of those that a mesh axis runs over, the one named last changes fastest.
Arguments:
- initial_state: float32 [2048, 256], P('batch'), may hold values from -6 to 6
- increments: float32 [32, 2048, 256], P('tm', 'batch'), may hold values from -1.5 to 1.5
- cotangents: float32 [32, 2048, 256], P('tm', 'batch'), may hold values from -1.5 to 1.5
- drift_inner: bfloat16 [256, 1024], replicated, may hold values from -0.375 to 0.375
- drift_hidden: float32 [1024], replicated, may hold values from -3 to 3
- drift_outer: bfloat16 [1024, 256], replicated, may hold values from -0.1875 to 0.1875
- drift_offset: float32 [256], replicated, may hold values from -3 to 3
- noise_inner: bfloat16 [256, 1024], replicated, may hold values from -0.375 to 0.375
- noise_hidden: float32 [1024], replicated, may hold values from -3 to 3
- noise_outer: bfloat16 [1024, 256], replicated, may hold values from -0.1875 to 0.1875
- noise_offset: float32 [256], replicated, may hold values from -4 to 4
Outputs:
- states: float32 [32, 2048, 256], P('tm', 'batch')
- adjoints: float32 [32, 2048, 256], P('tm', 'batch')
- drift_inner_grad: float32 [256, 1024], replicated
- drift_hidden_grad: float32 [1024], replicated
- drift_outer_grad: float32 [1024, 256], replicated
- drift_offset_grad: float32 [256], replicated
- noise_inner_grad: float32 [256, 1024], replicated
- noise_hidden_grad: float32 [1024], replicated
- noise_outer_grad: float32 [1024, 256], replicated
- noise_offset_grad: float32 [256], replicated
All inputs are finite; a program needn't handle non-finite values.
Results may differ from a plain program's by a relative error of at most 0.0095.
Values sent between devices are 32-bit elements; how exact they have to be, the bound alone decides.
No kernel may reach another device: no remote copies, remote signals or barrier semaphores. Data moves between devices by JAX's collectives and lax.ppermute only.
A program may use at most 128 MiB of HBM per device.

v0:
```python
import math
import jax
import jax.numpy as jnp
from jax import lax
from jax.sharding import PartitionSpec as P

L = 256
H = 1024
delta_time = 0.05


def shifted(block, axis, distance):
    devices = range(lax.axis_size(axis))
    route = [(i - distance, i) for i in devices if i - distance in devices]
    return lax.ppermute(block, axis, route)


def matmul(left, right):
    return jnp.dot(left, right, preferred_element_type=jnp.float32)


def matmul_transposed(left, right):
    return lax.dot_general(
        left, right, (((1,), (1,)), ((), ())), preferred_element_type=jnp.float32
    )


def matmul_rows(left, right):
    return lax.dot_general(
        left, right, (((0,), (0,)), ((), ())), preferred_element_type=jnp.float32
    )


def advance(state, noise, params):
    (
        drift_inner,
        drift_hidden,
        drift_outer,
        drift_offset,
        noise_inner,
        noise_hidden,
        noise_outer,
        noise_offset,
    ) = params
    state_low = state.astype(jnp.bfloat16)
    hidden_drift = jnp.tanh(matmul(state_low, drift_inner) + drift_hidden).astype(jnp.bfloat16)
    hidden_noise = jnp.tanh(matmul(state_low, noise_inner) + noise_hidden).astype(jnp.bfloat16)
    drift = matmul(hidden_drift, drift_outer) + drift_offset
    spread = jax.nn.sigmoid(matmul(hidden_noise, noise_outer) + noise_offset)
    return (
        state + delta_time * drift + spread * noise,
        (state_low, hidden_drift, hidden_noise, spread),
    )


def retreat(adjoint_next, state, noise, params):
    (
        drift_inner,
        drift_hidden,
        drift_outer,
        drift_offset,
        noise_inner,
        noise_hidden,
        noise_outer,
        noise_offset,
    ) = params
    unused, saved = advance(state, noise, params)
    state_low, hidden_drift, hidden_noise, spread = saved
    drift_grad = delta_time * adjoint_next
    noise_grad = adjoint_next * noise * spread * (1.0 - spread)
    drift_low = drift_grad.astype(jnp.bfloat16)
    noise_low = noise_grad.astype(jnp.bfloat16)
    back_drift = matmul_transposed(drift_low, drift_outer) * (
        1.0 - jnp.square(hidden_drift.astype(jnp.float32))
    )
    back_noise = matmul_transposed(noise_low, noise_outer) * (
        1.0 - jnp.square(hidden_noise.astype(jnp.float32))
    )
    back_drift_low = back_drift.astype(jnp.bfloat16)
    back_noise_low = back_noise.astype(jnp.bfloat16)
    adjoint = (
        adjoint_next
        + matmul_transposed(back_drift_low, drift_inner)
        + matmul_transposed(back_noise_low, noise_inner)
    )
    grads = (
        matmul_rows(state_low, back_drift_low),
        jnp.sum(back_drift, 0),
        matmul_rows(hidden_drift, drift_low),
        jnp.sum(drift_grad, 0),
        matmul_rows(state_low, back_noise_low),
        jnp.sum(back_noise, 0),
        matmul_rows(hidden_noise, noise_low),
        jnp.sum(noise_grad, 0),
    )
    return (adjoint, grads)


def squares(grads):
    total = jnp.sum(jnp.square(grads[0]))
    for entry in grads[1:]:
        total = total + jnp.sum(jnp.square(entry))
    return total


def clip_factor(total):
    limit = 0.5 * math.sqrt(4 * L * H + 2 * H + 2 * L)
    return jnp.minimum(1.0, limit / jnp.sqrt(total))


def shards(
    initial_state,
    increments,
    cotangents,
    drift_inner,
    drift_hidden,
    drift_outer,
    drift_offset,
    noise_inner,
    noise_hidden,
    noise_outer,
    noise_offset,
):
    params = (
        drift_inner,
        drift_hidden,
        drift_outer,
        drift_offset,
        noise_inner,
        noise_hidden,
        noise_outer,
        noise_offset,
    )
    segments = lax.axis_size("tm")
    segment = lax.axis_index("tm")
    steps_here, rows, width = increments.shape
    blocks = 2
    block_rows = rows // blocks
    rounds = blocks + segments - 1

    def run_forward(operand):
        start_state, block, states, entries = operand
        offset = block * block_rows
        noise_block = lax.dynamic_slice_in_dim(increments, offset, block_rows, 1)
        state = start_state
        produced = []
        for index in range(steps_here):
            state, unused = advance(state, noise_block[index], params)
            produced.append(state)
        states = lax.dynamic_update_slice_in_dim(states, jnp.stack(produced), offset, 1)
        entries = lax.dynamic_update_slice_in_dim(entries, start_state, offset, 0)
        return (state, states, entries)

    def skip_forward(operand):
        start_state, block, states, entries = operand
        return (jnp.zeros_like(start_state), states, entries)

    def forward_round(turn, carry):
        incoming, states, entries = carry
        block = turn - segment
        valid = (block >= 0) & (block < blocks)
        clamped = jnp.clip(block, 0, blocks - 1)
        own = lax.dynamic_slice_in_dim(initial_state, clamped * block_rows, block_rows, 0)
        start_state = jnp.where(segment == 0, own, incoming)
        outgoing, states, entries = lax.cond(
            valid, run_forward, skip_forward, (start_state, clamped, states, entries)
        )
        incoming = shifted(outgoing, "tm", 1)
        return (incoming, states, entries)

    start = (
        jnp.zeros((block_rows, width), jnp.float32),
        jnp.zeros_like(increments),
        jnp.zeros_like(initial_state),
    )
    unused, states, entries = lax.fori_loop(0, rounds, forward_round, start)

    def run_backward(operand):
        adjoint, block, adjoints, totals = operand
        offset = block * block_rows
        noise_block = lax.dynamic_slice_in_dim(increments, offset, block_rows, 1)
        cotangent_block = lax.dynamic_slice_in_dim(cotangents, offset, block_rows, 1)
        state_block = lax.dynamic_slice_in_dim(states, offset, block_rows, 1)
        entry = lax.dynamic_slice_in_dim(entries, offset, block_rows, 0)
        column = [None] * steps_here
        for index in reversed(range(steps_here)):
            before = entry if index == 0 else state_block[index - 1]
            adjoint, grads = retreat(
                adjoint + cotangent_block[index], before, noise_block[index], params
            )
            totals = tuple((a + b for a, b in zip(totals, grads)))
            column[index] = adjoint
        adjoints = lax.dynamic_update_slice_in_dim(adjoints, jnp.stack(column), offset, 1)
        return (adjoint, adjoints, totals)

    def skip_backward(operand):
        adjoint, block, adjoints, totals = operand
        return (jnp.zeros_like(adjoint), adjoints, totals)

    def backward_round(turn, carry):
        incoming, adjoints, totals = carry
        block = turn - (segments - 1 - segment)
        valid = (block >= 0) & (block < blocks)
        clamped = jnp.clip(block, 0, blocks - 1)
        outgoing, adjoints, totals = lax.cond(
            valid, run_backward, skip_backward, (incoming, clamped, adjoints, totals)
        )
        incoming = shifted(outgoing, "tm", -1)
        return (incoming, adjoints, totals)

    blank = tuple((jnp.zeros(p.shape, jnp.float32) for p in params))
    start = (jnp.zeros((block_rows, width), jnp.float32), jnp.zeros_like(increments), blank)
    unused, adjoints, totals = lax.fori_loop(0, rounds, backward_round, start)
    summed = lax.psum(
        (totals[0], totals[1], totals[2], totals[3], totals[4], totals[5], totals[6], totals[7]),
        ("tm", "batch"),
    )
    factor = clip_factor(squares(summed))
    result = tuple((entry * factor for entry in summed))
    return (
        states,
        adjoints,
        result[0],
        result[1],
        result[2],
        result[3],
        result[4],
        result[5],
        result[6],
        result[7],
    )


def solution(mesh):
    placed = (
        P("batch", None),
        P("tm", "batch", None),
        P("tm", "batch", None),
        P(),
        P(),
        P(),
        P(),
        P(),
        P(),
        P(),
        P(),
    )
    return jax.shard_map(
        shards,
        mesh=mesh,
        in_specs=placed,
        out_specs=(
            P("tm", "batch", None),
            P("tm", "batch", None),
            P(),
            P(),
            P(),
            P(),
            P(),
            P(),
            P(),
            P(),
        ),
        check_vma=False,
    )
```

profile of v0, /device:TPU:0, one launch (start us, length us, event | category | flops | bytes accessed | tf_op | source)
XLA Modules:
  0.0 786.6 jit_solution(2424366928954173790)
XLA Ops:
  9.5 93.3 %while.51 = (s32[]{:T(128)}, f32[128,256]{1,0:T(8,128)S(1)}, f32[8,256,256]{2,1,0:T(8,128)}, bf16[256,256]{1,0:T(8,128)(2,1)}, s32[]{:T(128)}, /*index=5*/pred[]...) while((s32[]{:T(128)}, f32[128,256]{1,0:T(8,128)S(1)}, ...), condition=%wide.region_3.4_spmd, body=%wide.region_0.3_spmd.sunk | while | flops 2154594304 | bytes 28394616 | solution.py:176
  9.5 17.4 %conditional.4 = (f32[128,256]{1,0:T(8,128)}, f32[8,256,256]{2,1,0:T(8,128)}, bf16[256,256]{1,0:T(8,128)(2,1)}) conditional(s32[]{:T(128)} %convert_element_type.851, (f32[8,256,256]{2,1,0:T(8,128)}, bf16[256,256]{1,0:T(8,128)(2,1)}) %tuple.170, (pred[]{:T(512)}, s32[]{:T(128)}, f32[256,256]{1,0:T(8,128)}, f32[128,256]{1,0:T(8,128)S(1)}, ...), branch_computations={%region_1.1_spmd, %region_2.2_spmd} | conditional | flops 2154594304 | bytes 27869942 | solution.py:165
  29.4 17.4 %conditional.4 = (f32[128,256]{1,0:T(8,128)}, f32[8,256,256]{2,1,0:T(8,128)}, bf16[256,256]{1,0:T(8,128)(2,1)}) conditional(s32[]{:T(128)} %convert_element_type.851, (f32[8,256,256]{2,1,0:T(8,128)}, bf16[256,256]{1,0:T(8,128)(2,1)}) %tuple.170, (pred[]{:T(512)}, s32[]{:T(128)}, f32[256,256]{1,0:T(8,128)}, f32[128,256]{1,0:T(8,128)S(1)}, ...), branch_computations={%region_1.1_spmd, %region_2.2_spmd} | conditional | flops 2154594304 | bytes 27869942 | solution.py:165
  46.8 2.3 collective-permute-start
  50.9 19.7 %collective-permute-start = (f32[128,256]{1,0:T(8,128)}, f32[128,256]{1,0:T(8,128)S(1)}, u32[]{:S(2)}, u32[]{:S(2)}) collective-permute-start(f32[128,256]{1,0:T(8,128)} %get-tuple-element.1600), channel_id=1, source_target_pairs={{0,8},{8,16},{16,24},{1,9},{9,17},{17,25},{2,10},{10,18},{18,26},{... | collective-permute-start | bytes 393224 | tf_op jit(solution)/shard_map/while/body/eval_jaxpr/ppermute | solution.py:15
  72.5 5.3 collective-permute-start
  79.6 22.0 %collective-permute-start = (f32[128,256]{1,0:T(8,128)}, f32[128,256]{1,0:T(8,128)S(1)}, u32[]{:S(2)}, u32[]{:S(2)}) collective-permute-start(f32[128,256]{1,0:T(8,128)} %get-tuple-element.1600), channel_id=1, source_target_pairs={{0,8},{8,16},{16,24},{1,9},{9,17},{17,25},{2,10},{10,18},{18,26},{... | collective-permute-start | bytes 393224 | tf_op jit(solution)/shard_map/while/body/eval_jaxpr/ppermute | solution.py:15
  102.8 2.7 convert.30
  112.6 504.2 %while.52 = (s32[]{:T(128)}, f32[128,256]{1,0:T(8,128)S(1)}, f32[8,256,256]{2,1,0:T(8,128)}, f32[256,1024]{1,0:T(8,128)S(1)}, f32[1024]{0:T(1024)}, /*index=5*/f...) while((s32[]{:T(128)}, f32[128,256]{1,0:T(8,128)S(1)}, ...), condition=%wide.region_39.40_spmd, body=%wide.region_4.39_spmd.sunk | while | flops 5935726592 | bytes 240598432 | solution.py:213
  114.6 5.1 collective-permute-done.1
  121.7 16.1 %collective-permute-done.1 = f32[128,256]{1,0:T(8,128)S(1)} collective-permute-done((f32[128,256]{1,0:T(8,128)}, f32[128,256]{1,0:T(8,128)S(1)}, u32[]{:S(2)}, u32[]{:S(2)}) %collective-permute-start.1) | collective-permute-done | bytes 131104 | tf_op jit(solution)/shard_map/while/body/eval_jaxpr/ppermute | solution.py:15
  139.7 280.0 %collective-permute-done.1 = f32[128,256]{1,0:T(8,128)S(1)} collective-permute-done((f32[128,256]{1,0:T(8,128)}, f32[128,256]{1,0:T(8,128)S(1)}, u32[]{:S(2)}, u32[]{:S(2)}) %collective-permute-start.1) | collective-permute-done | bytes 131104 | tf_op jit(solution)/shard_map/while/body/eval_jaxpr/ppermute | solution.py:15
  419.8 92.9 %conditional.5 = (f32[128,256]{1,0:T(8,128)S(1)}, f32[8,256,256]{2,1,0:T(8,128)}, f32[256,1024]{1,0:T(8,128)S(1)}, f32[1024]{0:T(1024)}, f32[1024,256]{1,0:T(8,1...) conditional(s32[]{:T(128)} %convert_element_type.852, ...), branch_computations={%region_5.5_spmd, %region_6.38_spmd} | conditional | flops 5935726592 | bytes 239549264 | solution.py:205
  428.0 2.5 multiply_reduce_fusion.6
  438.0 2.5 multiply_reduce_fusion.5
  448.2 2.6 multiply_reduce_fusion.4
  459.3 2.6 multiply_reduce_fusion.3
  470.4 2.6 multiply_reduce_fusion.2
  494.3 2.2 convolution_add_fusion.24
  514.6 5.2 collective-permute-done.1
  519.8 92.9 %conditional.5 = (f32[128,256]{1,0:T(8,128)S(1)}, f32[8,256,256]{2,1,0:T(8,128)}, f32[256,1024]{1,0:T(8,128)S(1)}, f32[1024]{0:T(1024)}, f32[1024,256]{1,0:T(8,1...) conditional(s32[]{:T(128)} %convert_element_type.852, ...), branch_computations={%region_5.5_spmd, %region_6.38_spmd} | conditional | flops 5935726592 | bytes 239549264 | solution.py:205
  528.1 2.5 multiply_reduce_fusion.6
  538.1 2.5 multiply_reduce_fusion.5
  548.3 2.6 multiply_reduce_fusion.4
  559.4 2.6 multiply_reduce_fusion.3
  570.5 2.6 multiply_reduce_fusion.2
  594.4 2.2 convolution_add_fusion.24
  614.7 2.1 collective-permute-done.1
  617.8 42.0 %all-reduce = (f32[1024]{0:T(1024)S(1)}, f32[256]{0:T(256)S(1)}, f32[1024]{0:T(1024)S(1)}, f32[256]{0:T(256)S(1)}) all-reduce(f32[1024]{0:T(1024)} %get-tuple-element.1132, f32[256]{0:T(256)} %get-tuple-element.1134, f32[1024]{0:T(1024)} %get-tuple-element.1136, ...), channel_id=1, replica_groups=mesh['tm'=4,'batch'=8] {'tm','batch'}, use_global_device_ids=true, to_apply=%region_42.43 | all-reduce | flops 2560 | bytes 20480 | tf_op jit(solution)/shard_map/psum | solution.py:214
  661.7 101.5 %all-reduce.4.cloned.1.call-done = (f32[256,1024]{1,0:T(8,128)}, f32[1024,256]{1,0:T(8,128)}, f32[256,1024]{1,0:T(8,128)}, f32[1024,256]{1,0:T(8,128)}) async-done(((f32[256,1024]{1,0:T(8,128)}, f32[1024,256]{1,0:T(8,128)}, f32[256,1024]{1,0:T(8,128)}, f32[1024,256]{1,0:T(8,128)}), (f32[256,1024]{1,0:T(8,128)}, f32[1024,256]{1,0:T(8,128)}, f32[256,1024]{1,0:T(8,128)}, ...) | async-done | bytes 4194320 | tf_op jit(solution)/shard_map/psum | solution.py:214
  763.2 2.6 multiply_reduce_fusion.8
  772.5 2.4 broadcast_multiply_fusion
  (621 shorter events, 227.5 us)
Async XLA Ops:
  7.2 756.0 %all-reduce.4.cloned.1.call-start = ((), (), s32[]{:S(2)}) async-start(), calls=%async_computation | async-start | bytes 8388608 | tf_op jit(solution)/shard_map/psum | solution.py:214
  27.0 2.5 collective-permute-start
  46.8 3.4 collective-permute-start
  50.9 20.9 %collective-permute-start = (f32[128,256]{1,0:T(8,128)}, f32[128,256]{1,0:T(8,128)S(1)}, u32[]{:S(2)}, u32[]{:S(2)}) collective-permute-start(f32[128,256]{1,0:T(8,128)} %get-tuple-element.1600), channel_id=1, source_target_pairs={{0,8},{8,16},{16,24},{1,9},{9,17},{17,25},{2,10},{10,18},{18,26},{... | collective-permute-start | bytes 393224 | tf_op jit(solution)/shard_map/while/body/eval_jaxpr/ppermute | solution.py:15
  72.5 6.5 collective-permute-start
  79.6 23.2 %collective-permute-start = (f32[128,256]{1,0:T(8,128)}, f32[128,256]{1,0:T(8,128)S(1)}, u32[]{:S(2)}, u32[]{:S(2)}) collective-permute-start(f32[128,256]{1,0:T(8,128)} %get-tuple-element.1600), channel_id=1, source_target_pairs={{0,8},{8,16},{16,24},{1,9},{9,17},{17,25},{2,10},{10,18},{18,26},{... | collective-permute-start | bytes 393224 | tf_op jit(solution)/shard_map/while/body/eval_jaxpr/ppermute | solution.py:15
  113.3 6.3 collective-permute-start.1
  120.4 17.4 %collective-permute-start.1 = (f32[128,256]{1,0:T(8,128)}, f32[128,256]{1,0:T(8,128)S(1)}, u32[]{:S(2)}, u32[]{:S(2)}) collective-permute-start(f32[128,256]{1,0:T(8,128)} %copy-done.65), channel_id=1, source_target_pairs={{8,0},{16,8},{24,16},{9,1},{17,9},{25,17},{10,2},{18,10},{26,18},{... | collective-permute-start | bytes 393224 | tf_op jit(solution)/shard_map/while/body/eval_jaxpr/ppermute | solution.py:15
  138.4 281.3 %collective-permute-start.1 = (f32[128,256]{1,0:T(8,128)}, f32[128,256]{1,0:T(8,128)S(1)}, u32[]{:S(2)}, u32[]{:S(2)}) collective-permute-start(f32[128,256]{1,0:T(8,128)} %copy-done.65), channel_id=1, source_target_pairs={{8,0},{16,8},{24,16},{9,1},{17,9},{25,17},{10,2},{18,10},{26,18},{... | collective-permute-start | bytes 393224 | tf_op jit(solution)/shard_map/while/body/eval_jaxpr/ppermute | solution.py:15
  428.0 4.6 copy-start.51
  428.0 4.6 copy-start.60
  430.5 6.4 copy-start.36
  440.5 6.0 copy-start.38
  448.2 4.6 copy-start.6
  450.9 6.8 copy-start.40
  459.3 4.7 copy-start.7
  462.0 6.8 copy-start.42
  470.4 4.6 copy-start.8
  473.1 6.8 copy-start.44
  513.3 6.5 collective-permute-start.1
  528.0 4.6 copy-start.51
  528.1 4.6 copy-start.60
  530.6 6.4 copy-start.36
  540.6 6.0 copy-start.38
  548.3 4.6 copy-start.6
  550.9 6.8 copy-start.40
  559.4 4.7 copy-start.7
  562.0 6.8 copy-start.42
  570.5 4.6 copy-start.8
  573.1 6.8 copy-start.44
  613.4 3.4 collective-permute-start.1
  772.5 4.6 copy-start.62
  (153 other events, 295.0 us)
Sparse Core Ops, SparseCore 0:
  618.0 145.2 all-reduce.3
where the time goes:
time: 789 us; the launch traced here: 787 us
  waiting for transfers between devices  416 us (53%)
  matrix products  175 us (22%)
  starting transfers between devices  57 us (7%)
  local copies, waits for them, and re-layouts  46.9 us (6%)
  blocking collectives  42 us (5%)
  other arithmetic  27.2 us (3%)
  between operations  19.4 us (2%)
    ppermute x10, waiting for transfers between devices, shifted(): return lax.ppermute(block, axis, route)  314 us
    psum x1, waiting for transfers between devices, shards(): lax.psum((totals[0], totals[1], totals[2], totals[3], totals[4], totals[5...  102 us
    dot_general x64, matrix products, matmul_transposed(): lax.dot_general(left, right, (((1,), (1,)), ((), ())), preferred_element_...  69.6 us
    dot_general x80, matrix products, matmul(): return jnp.dot(left, right, preferred_element_type=jnp.float32)  66.4 us
    ppermute x10, starting transfers between devices, shifted(): return lax.ppermute(block, axis, route)  57 us
    psum x1, blocking collectives, shards(): lax.psum((totals[0], totals[1], totals[2], totals[3], totals[4], totals[5...  42 us
    dot_general x64, matrix products, matmul_rows(): lax.dot_general(left, right, (((0,), (0,)), ((), ())), preferred_element_...  39.4 us
    cond x328, local copies, waits for them, and re-layouts  26.8 us
  transfers between devices with their start and end apart: 11, of which 11 were waited for; matrix products, arithmetic and copies ran while one was open for 0% of the time, Pallas kernels for 0%

commit v1 on v0

--- a/solution.py
+++ b/solution.py
@@ -212,8 +212,20 @@
     start = (jnp.zeros((block_rows, width), jnp.float32), jnp.zeros_like(increments), blank)
     unused, adjoints, totals = lax.fori_loop(0, rounds, backward_round, start)
     summed = lax.psum(
-        (totals[0], totals[1], totals[2], totals[3], totals[4], totals[5], totals[6], totals[7]),
-        ("tm", "batch"),
+        lax.psum(
+            (
+                totals[0],
+                totals[1],
+                totals[2],
+                totals[3],
+                totals[4],
+                totals[5],
+                totals[6],
+                totals[7],
+            ),
+            "batch",
+        ),
+        "tm",
     )
     factor = clip_factor(squares(summed))
     result = tuple((entry * factor for entry in summed))

time: 789 us -> 889 us (1.13)
  waiting for transfers between devices: 416 us -> 513 us
    psum x1, waiting for transfers between devices: 102 us -> 158 us  [shards(): lax.psum((totals[0], totals[1], totals[2], totals[3], totals[4], totals[5...]
    psum x0 -> x1, waiting for transfers between devices: none -> 39.8 us  [shards(): lax.psum(lax.psum((totals[0], totals[1], totals[2], totals[3], totals[4],...]
    psum x0 -> x1, blocking collectives: none -> 10.9 us  [shards(): lax.psum(lax.psum((totals[0], totals[1], totals[2], totals[3], totals[4],...]
  transfers between devices with their start and end apart: 11 -> 12, of which waited for: 11 -> 12; matrix products, arithmetic and copies ran while one was open for 0% -> 0% of each run, Pallas kernels for 0% -> 0%
where the time goes in v1:
time: 889 us; the launch traced here: 887 us
  waiting for transfers between devices  513 us (58%)
  matrix products  175 us (20%)
  starting transfers between devices  57.1 us (6%)
  local copies, waits for them, and re-layouts  46.9 us (5%)
  blocking collectives  45.8 us (5%)
  other arithmetic  27.1 us (3%)
  between operations  19.4 us (2%)
    ppermute x10, waiting for transfers between devices, shifted(): return lax.ppermute(block, axis, route)  314 us
    psum x1, waiting for transfers between devices, shards(): lax.psum((totals[0], totals[1], totals[2], totals[3], totals[4], totals[5...  158 us
    dot_general x64, matrix products, matmul_transposed(): lax.dot_general(left, right, (((1,), (1,)), ((), ())), preferred_element_...  69.6 us
    dot_general x80, matrix products, matmul(): return jnp.dot(left, right, preferred_element_type=jnp.float32)  66.4 us
    ppermute x10, starting transfers between devices, shifted(): return lax.ppermute(block, axis, route)  57 us
    psum x1, waiting for transfers between devices, shards(): lax.psum(lax.psum((totals[0], totals[1], totals[2], totals[3], totals[4],...  39.8 us
    dot_general x64, matrix products, matmul_rows(): lax.dot_general(left, right, (((0,), (0,)), ((), ())), preferred_element_...  39.4 us
    psum x1, blocking collectives, shards(): lax.psum((totals[0], totals[1], totals[2], totals[3], totals[4], totals[5...  34.9 us
  transfers between devices with their start and end apart: 12, of which 12 were waited for; matrix products, arithmetic and copies ran while one was open for 0% of the time, Pallas kernels for 0%

profile of v1, /device:TPU:0, one launch (start us, length us, event | category | flops | bytes accessed | tf_op | source)
XLA Modules:
  0.0 887.0 jit_solution(11368989560200339694)
XLA Ops:
  9.5 93.3 %while.51 = (s32[]{:T(128)}, f32[128,256]{1,0:T(8,128)S(1)}, f32[8,256,256]{2,1,0:T(8,128)}, bf16[256,256]{1,0:T(8,128)(2,1)}, s32[]{:T(128)}, /*index=5*/pred[]...) while((s32[]{:T(128)}, f32[128,256]{1,0:T(8,128)S(1)}, ...), condition=%wide.region_3.4_spmd, body=%wide.region_0.3_spmd.sunk | while | flops 2154594304 | bytes 28394616 | solution.py:176
  9.5 17.4 %conditional.4 = (f32[128,256]{1,0:T(8,128)}, f32[8,256,256]{2,1,0:T(8,128)}, bf16[256,256]{1,0:T(8,128)(2,1)}) conditional(s32[]{:T(128)} %convert_element_type.851, (f32[8,256,256]{2,1,0:T(8,128)}, bf16[256,256]{1,0:T(8,128)(2,1)}) %tuple.170, (pred[]{:T(512)}, s32[]{:T(128)}, f32[256,256]{1,0:T(8,128)}, f32[128,256]{1,0:T(8,128)S(1)}, ...), branch_computations={%region_1.1_spmd, %region_2.2_spmd} | conditional | flops 2154594304 | bytes 27869942 | solution.py:165
  29.4 17.4 %conditional.4 = (f32[128,256]{1,0:T(8,128)}, f32[8,256,256]{2,1,0:T(8,128)}, bf16[256,256]{1,0:T(8,128)(2,1)}) conditional(s32[]{:T(128)} %convert_element_type.851, (f32[8,256,256]{2,1,0:T(8,128)}, bf16[256,256]{1,0:T(8,128)(2,1)}) %tuple.170, (pred[]{:T(512)}, s32[]{:T(128)}, f32[256,256]{1,0:T(8,128)}, f32[128,256]{1,0:T(8,128)S(1)}, ...), branch_computations={%region_1.1_spmd, %region_2.2_spmd} | conditional | flops 2154594304 | bytes 27869942 | solution.py:165
  46.8 2.3 collective-permute-start
  50.9 19.7 %collective-permute-start = (f32[128,256]{1,0:T(8,128)}, f32[128,256]{1,0:T(8,128)S(1)}, u32[]{:S(2)}, u32[]{:S(2)}) collective-permute-start(f32[128,256]{1,0:T(8,128)} %get-tuple-element.1608), channel_id=1, source_target_pairs={{0,8},{8,16},{16,24},{1,9},{9,17},{17,25},{2,10},{10,18},{18,26},{... | collective-permute-start | bytes 393224 | tf_op jit(solution)/shard_map/while/body/eval_jaxpr/ppermute | solution.py:15
  72.5 5.3 collective-permute-start
  79.6 22.0 %collective-permute-start = (f32[128,256]{1,0:T(8,128)}, f32[128,256]{1,0:T(8,128)S(1)}, u32[]{:S(2)}, u32[]{:S(2)}) collective-permute-start(f32[128,256]{1,0:T(8,128)} %get-tuple-element.1608), channel_id=1, source_target_pairs={{0,8},{8,16},{16,24},{1,9},{9,17},{17,25},{2,10},{10,18},{18,26},{... | collective-permute-start | bytes 393224 | tf_op jit(solution)/shard_map/while/body/eval_jaxpr/ppermute | solution.py:15
  102.8 2.7 convert.30
  112.6 504.2 %while.52 = (s32[]{:T(128)}, f32[128,256]{1,0:T(8,128)S(1)}, f32[8,256,256]{2,1,0:T(8,128)}, f32[256,1024]{1,0:T(8,128)S(1)}, f32[1024]{0:T(1024)}, /*index=5*/f...) while((s32[]{:T(128)}, f32[128,256]{1,0:T(8,128)S(1)}, ...), condition=%wide.region_39.40_spmd, body=%wide.region_4.39_spmd.sunk | while | flops 5935726592 | bytes 240598432 | solution.py:213
  114.6 5.1 collective-permute-done.1
  121.7 16.1 %collective-permute-done.1 = f32[128,256]{1,0:T(8,128)S(1)} collective-permute-done((f32[128,256]{1,0:T(8,128)}, f32[128,256]{1,0:T(8,128)S(1)}, u32[]{:S(2)}, u32[]{:S(2)}) %collective-permute-start.1) | collective-permute-done | bytes 131104 | tf_op jit(solution)/shard_map/while/body/eval_jaxpr/ppermute | solution.py:15
  139.7 280.0 %collective-permute-done.1 = f32[128,256]{1,0:T(8,128)S(1)} collective-permute-done((f32[128,256]{1,0:T(8,128)}, f32[128,256]{1,0:T(8,128)S(1)}, u32[]{:S(2)}, u32[]{:S(2)}) %collective-permute-start.1) | collective-permute-done | bytes 131104 | tf_op jit(solution)/shard_map/while/body/eval_jaxpr/ppermute | solution.py:15
  419.8 92.9 %conditional.5 = (f32[128,256]{1,0:T(8,128)S(1)}, f32[8,256,256]{2,1,0:T(8,128)}, f32[256,1024]{1,0:T(8,128)S(1)}, f32[1024]{0:T(1024)}, f32[1024,256]{1,0:T(8,1...) conditional(s32[]{:T(128)} %convert_element_type.852, ...), branch_computations={%region_5.5_spmd, %region_6.38_spmd} | conditional | flops 5935726592 | bytes 239549264 | solution.py:205
  428.0 2.5 multiply_reduce_fusion.6
  438.0 2.5 multiply_reduce_fusion.5
  448.2 2.6 multiply_reduce_fusion.4
  459.3 2.6 multiply_reduce_fusion.3
  470.4 2.6 multiply_reduce_fusion.2
  514.6 5.2 collective-permute-done.1
  519.8 92.9 %conditional.5 = (f32[128,256]{1,0:T(8,128)S(1)}, f32[8,256,256]{2,1,0:T(8,128)}, f32[256,1024]{1,0:T(8,128)S(1)}, f32[1024]{0:T(1024)}, f32[1024,256]{1,0:T(8,1...) conditional(s32[]{:T(128)} %convert_element_type.852, ...), branch_computations={%region_5.5_spmd, %region_6.38_spmd} | conditional | flops 5935726592 | bytes 239549264 | solution.py:205
  528.1 2.5 multiply_reduce_fusion.6
  538.1 2.5 multiply_reduce_fusion.5
  548.3 2.6 multiply_reduce_fusion.4
  559.4 2.6 multiply_reduce_fusion.3
  570.5 2.6 multiply_reduce_fusion.2
  594.4 2.2 convolution_add_fusion.24
  617.9 158.4 %all-reduce.7.cloned.1.call-done = (f32[256,1024]{1,0:T(8,128)}, f32[1024,256]{1,0:T(8,128)}, f32[256,1024]{1,0:T(8,128)}, f32[1024,256]{1,0:T(8,128)}) async-done(((f32[256,1024]{1,0:T(8,128)}, f32[1024,256]{1,0:T(8,128)}, f32[256,1024]{1,0:T(8,128)}, f32[1024,256]{1,0:T(8,128)}), (f32[256,1024]{1,0:T(8,128)}, f32[1024,256]{1,0:T(8,128)}, f32[256,1024]{1,0:T(8,128)}, ...) | async-done | bytes 4194320 | tf_op jit(solution)/shard_map/psum | solution.py:215
  776.3 34.9 %all-reduce = (f32[1024]{0:T(1024)S(1)}, f32[256]{0:T(256)S(1)}, f32[1024]{0:T(1024)S(1)}, f32[256]{0:T(256)S(1)}) all-reduce(f32[1024]{0:T(1024)} %get-tuple-element.1132, f32[256]{0:T(256)} %get-tuple-element.1134, f32[1024]{0:T(1024)} %get-tuple-element.1136, f32[256]{0:T(256)} %get-tuple-element.1138), channel_id=1, replica_groups=mesh['tm'=4,'batch'=8] {'batch'}, use_global_device_ids=true, to_apply=%region_43.44 | all-reduce | flops 2560 | bytes 20480 | tf_op jit(solution)/shard_map/psum | solution.py:215
  811.2 10.9 %all-reduce.2 = (f32[1024]{0:T(1024)S(1)}, f32[256]{0:T(256)S(1)}, f32[1024]{0:T(1024)S(1)}, f32[256]{0:T(256)S(1)}) all-reduce(f32[1024]{0:T(1024)S(1)} %get-tuple-element.1217, f32[256]{0:T(256)S(1)} %get-tuple-element.1218, f32[1024]{0:T(1024)S(1)} %get-tuple-element.1219, ...), channel_id=1, replica_groups=mesh['tm'=4,'batch'=8] {'tm'}, use_global_device_ids=true, to_apply=%region_44.45 | all-reduce | flops 2560 | bytes 20480 | tf_op jit(solution)/shard_map/psum | solution.py:214
  823.9 39.8 %all-reduce.9.cloned.1.call-done = (f32[256,1024]{1,0:T(8,128)}, f32[1024,256]{1,0:T(8,128)}, f32[256,1024]{1,0:T(8,128)}, f32[1024,256]{1,0:T(8,128)}) async-done(((f32[256,1024]{1,0:T(8,128)}, f32[1024,256]{1,0:T(8,128)}, f32[256,1024]{1,0:T(8,128)}, f32[1024,256]{1,0:T(8,128)}), (f32[256,1024]{1,0:T(8,128)}, f32[1024,256]{1,0:T(8,128)}, f32[256,1024]{1,0:T(8,128)}, ...) | async-done | bytes 4194320 | tf_op jit(solution)/shard_map/psum | solution.py:214
  863.7 2.6 multiply_reduce_fusion.8
  872.9 2.4 broadcast_multiply_fusion
  (625 shorter events, 231.8 us)
Async XLA Ops:
  7.2 769.0 %all-reduce.7.cloned.1.call-start = ((), (), s32[]{:S(2)}) async-start(), calls=%async_computation | async-start | bytes 8388608 | tf_op jit(solution)/shard_map/psum | solution.py:215
  27.0 2.5 collective-permute-start
  46.8 3.4 collective-permute-start
  50.9 20.9 %collective-permute-start = (f32[128,256]{1,0:T(8,128)}, f32[128,256]{1,0:T(8,128)S(1)}, u32[]{:S(2)}, u32[]{:S(2)}) collective-permute-start(f32[128,256]{1,0:T(8,128)} %get-tuple-element.1608), channel_id=1, source_target_pairs={{0,8},{8,16},{16,24},{1,9},{9,17},{17,25},{2,10},{10,18},{18,26},{... | collective-permute-start | bytes 393224 | tf_op jit(solution)/shard_map/while/body/eval_jaxpr/ppermute | solution.py:15
  72.5 6.5 collective-permute-start
  79.6 23.2 %collective-permute-start = (f32[128,256]{1,0:T(8,128)}, f32[128,256]{1,0:T(8,128)S(1)}, u32[]{:S(2)}, u32[]{:S(2)}) collective-permute-start(f32[128,256]{1,0:T(8,128)} %get-tuple-element.1608), channel_id=1, source_target_pairs={{0,8},{8,16},{16,24},{1,9},{9,17},{17,25},{2,10},{10,18},{18,26},{... | collective-permute-start | bytes 393224 | tf_op jit(solution)/shard_map/while/body/eval_jaxpr/ppermute | solution.py:15
  113.3 6.3 collective-permute-start.1
  120.4 17.4 %collective-permute-start.1 = (f32[128,256]{1,0:T(8,128)}, f32[128,256]{1,0:T(8,128)S(1)}, u32[]{:S(2)}, u32[]{:S(2)}) collective-permute-start(f32[128,256]{1,0:T(8,128)} %copy-done.65), channel_id=1, source_target_pairs={{8,0},{16,8},{24,16},{9,1},{17,9},{25,17},{10,2},{18,10},{26,18},{... | collective-permute-start | bytes 393224 | tf_op jit(solution)/shard_map/while/body/eval_jaxpr/ppermute | solution.py:15
  138.4 281.3 %collective-permute-start.1 = (f32[128,256]{1,0:T(8,128)}, f32[128,256]{1,0:T(8,128)S(1)}, u32[]{:S(2)}, u32[]{:S(2)}) collective-permute-start(f32[128,256]{1,0:T(8,128)} %copy-done.65), channel_id=1, source_target_pairs={{8,0},{16,8},{24,16},{9,1},{17,9},{25,17},{10,2},{18,10},{26,18},{... | collective-permute-start | bytes 393224 | tf_op jit(solution)/shard_map/while/body/eval_jaxpr/ppermute | solution.py:15
  428.0 4.6 copy-start.51
  428.0 4.6 copy-start.60
  430.5 6.4 copy-start.36
  440.5 6.0 copy-start.38
  448.2 4.6 copy-start.6
  450.9 6.8 copy-start.40
  459.3 4.7 copy-start.7
  462.0 6.8 copy-start.42
  470.4 4.6 copy-start.8
  473.1 6.8 copy-start.44
  513.3 6.5 collective-permute-start.1
  528.0 4.6 copy-start.51
  528.1 4.6 copy-start.60
  530.6 6.4 copy-start.36
  540.6 6.0 copy-start.38
  548.3 4.6 copy-start.6
  550.9 6.8 copy-start.40
  559.4 4.7 copy-start.7
  562.0 6.8 copy-start.42
  570.5 4.6 copy-start.8
  573.1 6.8 copy-start.44
  613.4 3.4 collective-permute-start.1
  617.8 245.8 %all-reduce.9.cloned.1.call-start = ((), (), s32[]{:S(2)}) async-start(), calls=%async_computation.1 | async-start | bytes 8388608 | tf_op jit(solution)/shard_map/psum | solution.py:214
  (154 other events, 299.5 us)
Sparse Core Ops, SparseCore 0:
  618.0 158.2 all-reduce.6
  778.8 84.7 all-reduce.8
